TPU v7x, 128 devices: a whole 4x4x4 slice. The times are simulated.
128 devices in a mesh: member: 2 (over x_lo), fsdp: 64 (over z, y, x_hi, core).
Axes of the slice: x: 4 (x_hi: 2, x_lo: 2; x = x_hi * 2 + x_lo), y: 4, z: 4, core: 2. Of those that a mesh axis runs over, the one named last changes fastest.
Arguments:
- latents: bfloat16 [2, 131072, 512], P('member', 'fsdp'), may hold values from -16 to 16
- noise: float32 [2, 32], P('member'), may hold values from -4 to 4
- cond_gain: float32 [32, 512], replicated, may hold values from -0.5 to 0.5
- cond_shift: float32 [32, 512], replicated, may hold values from -0.5 to 0.5
- w_in: bfloat16 [512, 2048], P('fsdp'), may hold values from -0.25 to 0.25
- b_in: float32 [2048], replicated, may hold values from -3 to 3
- w_out: bfloat16 [2048, 512], P('fsdp'), may hold values from -0.125 to 0.125
- target: bfloat16 [131072, 512], P('fsdp'), may hold values from -6 to 6
Outputs:
- prediction: bfloat16 [2, 131072, 512], P('member', 'fsdp')
- grad_in: float32 [512, 2048], P('fsdp')
- grad_out: float32 [2048, 512], P('fsdp')
- crps_mean: float32 [], replicated
All inputs are finite; a program needn't handle non-finite values.
Results may differ from a plain program's by a relative error of at most 0.0043.
Values may be sent and summed in bfloat16 or wider, within the bound.
A program may use at most 128 MiB of HBM per device.

v0:
```python
import functools
import jax
import jax.numpy as jnp
from jax import lax
from jax.sharding import Mesh
from jax.sharding import PartitionSpec as P

FSDP = ("fsdp_0", "fsdp_1", "fsdp_2", "fsdp_3")
MEMBER_FSDP = ("member", "fsdp_0", "fsdp_1", "fsdp_2", "fsdp_3")
COEF = 0.7978845608
CUBIC = 0.044715


def swapped(block, axis, apart):
    count = lax.axis_size(axis)
    route = []
    for low in range(count):
        high = low | 1 << apart
        if high != low and high < count:
            route += [(low, high), (high, low)]
    return lax.ppermute(block, axis, route)


def over_axes(x, axes):
    return functools.reduce(lax.psum, axes, x)


def total_of_pieces(x, axis):
    return lax.all_gather(x, axis).astype(jnp.float32).sum(0)


def in_blocks(x, dim, count):
    before, after = (x.shape[:dim], x.shape[dim + 1 :])
    return jnp.moveaxis(x.reshape(*before, count, -1, *after), dim, 0)


def sum_at_owner(x, axis, dim):
    count = lax.axis_size(axis)
    tiles = lax.all_to_all(in_blocks(x, dim, count), axis, 0, 0, tiled=True)
    return jnp.sum(tiles.astype(jnp.float32), axis=0)


def gelu_value(v):
    return 0.5 * v * (1.0 + jnp.tanh(COEF * (v + CUBIC * v * v * v)))


def gelu_slope(v):
    u = jnp.tanh(COEF * (v + CUBIC * v * v * v))
    return 0.5 * (1.0 + u) + 0.5 * v * (1.0 - u * u) * COEF * (1.0 + 3.0 * CUBIC * v * v)


def smooth(d):
    return jnp.sqrt(d * d + 0.0625)


def on_device(latents, noise, cond_gain, cond_shift, w_in, b_in, w_out, target):
    block = latents[0]
    noise_row = noise[0]
    rows = block.shape[0]
    width = block.shape[1]
    groups = lax.axis_size(FSDP)
    nodes = rows * groups
    gain = (
        1.0
        + jnp.dot(
            noise_row[None, :],
            cond_gain,
            precision=lax.Precision.HIGHEST,
            preferred_element_type=jnp.float32,
        )[0]
    )
    shift = jnp.dot(
        noise_row[None, :],
        cond_shift,
        precision=lax.Precision.HIGHEST,
        preferred_element_type=jnp.float32,
    )[0]
    values = block.astype(jnp.float32)
    center = jnp.mean(values, axis=1, keepdims=True)
    spread = jnp.mean((values - center) ** 2, axis=1, keepdims=True)
    normed = ((values - center) / jnp.sqrt(spread + 0.25) * gain + shift).astype(jnp.bfloat16)
    columns = normed
    pre = (
        jnp.dot(
            columns,
            lax.all_gather(w_in, FSDP, axis=0, tiled=True),
            preferred_element_type=jnp.float32,
        )
        + b_in
    )
    act = gelu_value(pre).astype(jnp.bfloat16)
    columns = act
    output = values + jnp.dot(
        columns, lax.all_gather(w_out, FSDP, axis=0, tiled=True), preferred_element_type=jnp.float32
    )
    prediction = output.astype(jnp.bfloat16)
    partner = swapped(prediction, "member", 0)
    mine = prediction.astype(jnp.float32)
    near = mine - target.astype(jnp.float32)
    apart = mine - partner.astype(jnp.float32)
    local_sum = jnp.sum(0.5 * smooth(near) - 0.25 * smooth(apart))
    crps_mean = over_axes(local_sum, MEMBER_FSDP) / jnp.float32(2 * nodes * width)
    scale = 1.0 / jnp.sqrt(jnp.float32(2 * nodes))
    dpred = ((0.5 * near / smooth(near) - 0.5 * apart / smooth(apart)) * scale).astype(jnp.bfloat16)
    across = (((1,), (1,)), ((), ()))
    dact = lax.dot_general(
        dpred,
        lax.all_gather(w_out, FSDP, axis=0, tiled=True),
        across,
        preferred_element_type=jnp.float32,
    )
    dpre = (dact * gelu_slope(pre)).astype(jnp.bfloat16)
    contract = (((0,), (0,)), ((), ()))
    full_in = lax.dot_general(normed, dpre, contract, preferred_element_type=jnp.float32)
    full_out = lax.dot_general(act, dpred, contract, preferred_element_type=jnp.float32)
    paired_in, paired_out = (
        total_of_pieces(full_in.astype(jnp.bfloat16), "member").astype(jnp.float32),
        total_of_pieces(full_out.astype(jnp.bfloat16), "member").astype(jnp.float32),
    )
    grad_in, grad_out = (
        sum_at_owner(paired_in.astype(jnp.bfloat16), FSDP, 0),
        sum_at_owner(paired_out.astype(jnp.bfloat16), FSDP, 0),
    )
    return (prediction[None], grad_in, grad_out, crps_mean)


def solution(mesh):
    torus = Mesh(
        mesh.devices.reshape(mesh.shape["member"], 4, 4, 2, 2),
        ("member", "fsdp_0", "fsdp_1", "fsdp_2", "fsdp_3"),
    )
    in_specs = (
        P("member", FSDP, None),
        P("member", None),
        P(),
        P(),
        P(FSDP, None),
        P(),
        P(FSDP, None),
        P(FSDP, None),
    )
    out_specs = (P("member", FSDP, None), P(FSDP, None), P(FSDP, None), P())
    return jax.shard_map(
        on_device, mesh=torus, in_specs=in_specs, out_specs=out_specs, check_vma=False
    )
```

profile of v0, /device:TPU:1, one launch (start us, length us, event | category | flops | bytes accessed | tf_op | source)
XLA Modules:
  0.0 460.8 jit_solution(7178948828208920969)
XLA Ops:
  7.3 0.7 all-gather.7.cloned.1.call-update
  8.0 0.7 all-gather.9.cloned.1.call-update
  8.7 0.0 all-gather.11.cloned.1.call-start
  8.8 1.9 convert_reduce_fusion
  10.7 0.8 fusion.20
  11.5 2.5 fusion.12
  14.1 0.1 fusion.18
  14.2 68.7 %all-gather.7.cloned.1.call-done = bf16[512,2048]{1,0:T(8,128)(2,1)} async-done(((bf16[8,2048]{1,0:T(8,128)(2,1)}), bf16[512,2048]{1,0:T(8,128)(2,1)}) %all-gather.7.cloned.1.call-update) | async-done | bytes 2097168 | tf_op jit(solution)/shard_map/all_gather | solution.py:86
  82.9 13.7 %multiply_convert_fusion = (bf16[2048,2048]{1,0:T(8,128)(2,1)}, f32[2048,2048]{1,0:T(8,128)}) fusion(f32[2048]{0:T(1024)S(1)} %copy-done.6, bf16[512,2048]{1,0:T(8,128)(2,1)} %all-gather.7.cloned.1.call-done, bf16[1,2048,512]{2,1,0:T(8,128)(2,1)S(1)} %copy-done.1, f32[512]{0:T(512)S(1)} %bitcast.49, f32[512]{0:T(512)S(1)} %broadcast_add_fusion, ...), kind=kOutput, calls=%fused_computation.9 | convolution fusion | flops 4343201792 | bytes 29388800 | tf_op jit(solution)/shard_map/dot_general | solution.py:84
  96.6 54.5 %all-gather.9.cloned.1.call-done = bf16[2048,512]{1,0:T(8,128)(2,1)} async-done(((bf16[32,512]{1,0:T(8,128)(2,1)}), bf16[2048,512]{1,0:T(8,128)(2,1)}) %all-gather.9.cloned.1.call-update) | async-done | bytes 2097168 | tf_op jit(solution)/shard_map/all_gather | solution.py:94
  151.1 8.5 %fusion.16 = bf16[2048,512]{1,0:T(8,128)(2,1)S(1)} fusion(bf16[1,2048,512]{2,1,0:T(8,128)(2,1)S(1)} %copy-done.1, bf16[2048,2048]{1,0:T(8,128)(2,1)} %get-tuple-element.4, bf16[2048,512]{1,0:T(8,128)(2,1)} %all-gather.9.cloned.1.call-done), kind=kOutput, calls=%fused_computation.23 | convolution fusion | flops 4298113024 | bytes 14680064 | tf_op jit(solution)/shard_map/dot_general | solution.py:93
  159.6 1.3 copy-done.2
  160.9 0.3 collective-permute-start
  161.2 46.6 %collective-permute-done = bf16[2048,512]{1,0:T(8,128)(2,1)S(1)} collective-permute-done((bf16[2048,512]{1,0:T(8,128)(2,1)S(1)}, bf16[2048,512]{1,0:T(8,128)(2,1)S(1)}, u32[]{:S(2)}, u32[]{:S(2)}) %collective-permute-start) | collective-permute-done | bytes 2097184 | tf_op jit(solution)/shard_map/ppermute | solution.py:21
  207.8 1.4 copy-done.3
  209.2 26.8 %fusion.17 = bf16[512,2048]{1,0:T(8,128)(2,1)} fusion(f32[2048,2048]{1,0:T(8,128)} %get-tuple-element.5, bf16[2048,512]{1,0:T(8,128)(2,1)} %all-gather.9.cloned.1.call-done, f32[2048]{0:T(1024)S(1)} %copy-done.6, bf16[1,2048,512]{2,1,0:T(8,128)(2,1)S(1)} %copy-done.1, f32[512]{0:T(512)S(1)} %bitcast.50, f32[512]{0:T(512)S(1)} %broadcast_add_fusion, ...), kind=kOutput, calls=%fused_computation.30 | convolution fusion | flops 8697937920 | bytes 29388800 | tf_op jit(solution)/shard_map/dot_general | solution.py:114
  236.0 0.3 all-gather.13.cloned.1.call-start
  236.3 13.9 %convolution_convert_fusion = bf16[2048,512]{1,0:T(8,128)(2,1)} fusion(bf16[2048,2048]{1,0:T(8,128)(2,1)} %get-tuple-element.4, bf16[2048,512]{1,0:T(8,128)(2,1)} %param.15, bf16[2048,512]{1,0:T(8,128)(2,1)} %copy-done.2, bf16[2048,512]{1,0:T(8,128)(2,1)} %copy-done.3), kind=kOutput, calls=%fused_computation.31 | convolution fusion | flops 4312793088 | bytes 16777216 | tf_op jit(solution)/shard_map/dot_general | solution.py:115
  250.3 42.4 %all-gather.11.cloned.1.call-done = bf16[1024,2048]{1,0:T(8,128)(2,1)} async-done(((bf16[512,2048]{1,0:T(8,128)(2,1)}), bf16[1024,2048]{1,0:T(8,128)(2,1)}) %all-gather.11.cloned.1.call-update) | async-done | bytes 4194320 | tf_op jit(solution)/shard_map/all_gather | solution.py:29
  292.6 5.1 %reduce_sum.71 = bf16[512,2048]{1,0:T(8,128)(2,1)} reduce(bf16[2,512,2048]{2,1,0:T(8,128)(2,1)} %bitcast.45, bf16[]{:T(256)} %constant.28.clone.1), dimensions={0}, to_apply=%region_2.0 | reduce | flops 1048576 | bytes 6291458 | tf_op jit(solution)/shard_map/reduce_sum | solution.py:29
  297.7 10.4 %all-to-all-start = ((bf16[64,8,2048]{2,1,0:T(8,128)(2,1)}), bf16[64,8,2048]{2,1,0:T(8,128)(2,1)S(1)}, u32[]{:S(2)}, u32[]{:S(2)}) async-start(bf16[64,8,2048]{2,1,0:T(8,128)(2,1)} %bitcast.8), calls=%async_computation | async-start | bytes 4194304 | tf_op jit(solution)/shard_map/all_to_all | solution.py:39
  308.1 68.6 %all-gather.13.cloned.1.call-done = bf16[4096,512]{1,0:T(8,128)(2,1)} async-done(((bf16[2048,512]{1,0:T(8,128)(2,1)}), bf16[4096,512]{1,0:T(8,128)(2,1)}) %all-gather.13.cloned.1.call-update) | async-done | bytes 4194320 | tf_op jit(solution)/shard_map/all_gather | solution.py:29
  376.6 5.0 %reduce_sum.73 = bf16[2048,512]{1,0:T(8,128)(2,1)} reduce(bf16[2,2048,512]{2,1,0:T(8,128)(2,1)} %bitcast.46, bf16[]{:T(256)} %constant.28.clone.1), dimensions={0}, to_apply=%region_4.0 | reduce | flops 1048576 | bytes 6291458 | tf_op jit(solution)/shard_map/reduce_sum | solution.py:29
  381.6 10.8 %all-to-all-start.1 = ((bf16[64,32,512]{2,1,0:T(8,128)(2,1)}), bf16[64,32,512]{2,1,0:T(8,128)(2,1)}, u32[]{:S(2)}, u32[]{:S(2)}) async-start(bf16[64,32,512]{2,1,0:T(8,128)(2,1)} %bitcast.10), calls=%async_computation.1 | async-start | bytes 4194304 | tf_op jit(solution)/shard_map/all_to_all | solution.py:39
  392.4 7.1 %subtract_reduce_fusion = f32[]{:T(128)} fusion(bf16[2048,512]{1,0:T(8,128)(2,1)} %param.15, bf16[2048,512]{1,0:T(8,128)(2,1)} %copy-done.2, bf16[2048,512]{1,0:T(8,128)(2,1)} %copy-done.3), kind=kLoop, calls=%fused_computation.24 | loop fusion | flops 13631487 | bytes 6291460 | tf_op jit(solution)/shard_map/reduce_sum | solution.py:101
  399.5 16.4 %psum.35 = f32[]{:T(128)} all-reduce(f32[]{:T(128)} %subtract_reduce_fusion), channel_id=1, replica_groups=mesh['member'=2,'fsdp_0'=4,'fsdp_1'=4,'fsdp_2'=2,'fsdp_3'=2] {'member'}, use_global_device_ids=true, to_apply=%region_7.0 | all-reduce | flops 1 | bytes 8 | tf_op jit(solution)/shard_map/psum | solution.py:25
  415.9 9.4 %psum.36 = f32[]{:T(128)} all-reduce(f32[]{:T(128)} %psum.35), channel_id=1, replica_groups=mesh['member'=2,'fsdp_0'=4,'fsdp_1'=4,'fsdp_2'=2,'fsdp_3'=2] {'fsdp_0'}, use_global_device_ids=true, to_apply=%region_8.0 | all-reduce | flops 1 | bytes 8 | tf_op jit(solution)/shard_map/psum | solution.py:25
  425.3 9.0 %psum.37 = f32[]{:T(128)} all-reduce(f32[]{:T(128)} %psum.36), channel_id=1, replica_groups=mesh['member'=2,'fsdp_0'=4,'fsdp_1'=4,'fsdp_2'=2,'fsdp_3'=2] {'fsdp_1'}, use_global_device_ids=true, to_apply=%region_9.0 | all-reduce | flops 1 | bytes 8 | tf_op jit(solution)/shard_map/psum | solution.py:25
  434.3 6.2 %psum.38 = f32[]{:T(128)} all-reduce(f32[]{:T(128)} %psum.37), channel_id=1, replica_groups=mesh['member'=2,'fsdp_0'=4,'fsdp_1'=4,'fsdp_2'=2,'fsdp_3'=2] {'fsdp_2'}, use_global_device_ids=true, to_apply=%region_10.0 | all-reduce | flops 1 | bytes 8 | tf_op jit(solution)/shard_map/psum | solution.py:25
  440.5 8.5 %psum.39 = f32[]{:T(128)} all-reduce(f32[]{:T(128)} %psum.38), channel_id=1, replica_groups=mesh['member'=2,'fsdp_0'=4,'fsdp_1'=4,'fsdp_2'=2,'fsdp_3'=2] {'fsdp_3'}, use_global_device_ids=true, to_apply=%region_11.0 | all-reduce | flops 1 | bytes 8 | tf_op jit(solution)/shard_map/psum | solution.py:25
  449.7 0.9 convert_reduce_fusion.2
  450.6 2.5 convert_reduce_fusion.1
  (21 shorter events, 0.2 us)
Async XLA Ops:
  7.2 3.5 copy-start
  7.2 75.7 %copy-start.1 = (bf16[1,2048,512]{2,1,0:T(8,128)(2,1)S(1)}, bf16[1,2048,512]{2,1,0:T(8,128)(2,1)}, u32[]{:S(2)}) copy-start(bf16[1,2048,512]{2,1,0:T(8,128)(2,1)} %param.8) | copy-start | bytes 6291460
  7.2 6.9 %copy-start.5 = (f32[1,32]{1,0:T(1,128)S(1)}, f32[1,32]{1,0:T(1,128)}, u32[]{:S(2)}) copy-start(f32[1,32]{1,0:T(1,128)} %param.9) | copy-start | bytes 388
  7.2 6.8 %copy-start.4 = (f32[32,512]{1,0:T(8,128)S(1)}, f32[32,512]{1,0:T(8,128)}, u32[]{:S(2)}) copy-start(f32[32,512]{1,0:T(8,128)} %param.11) | copy-start | bytes 196612
  7.2 75.7 %copy-start.6 = (f32[2048]{0:T(1024)S(1)}, f32[2048]{0:T(1024)}, u32[]{:S(2)}) copy-start(f32[2048]{0:T(1024)} %param.13) | copy-start | bytes 24580
  7.2 75.7 %all-gather.7.cloned.1.call-start = ((), (), s32[]{:S(2)}) async-start(), calls=%async_computation.2 | async-start | bytes 2129920 | tf_op jit(solution)/shard_map/all_gather | solution.py:86
  8.0 143.1 %all-gather.9.cloned.1.call-start = ((), (), s32[]{:S(2)}) async-start(), calls=%async_computation.3 | async-start | bytes 2129920 | tf_op jit(solution)/shard_map/all_gather | solution.py:94
  8.7 283.9 %all-gather.11.cloned.1.call-start = ((), (), s32[]{:S(2)}) async-start(), calls=%async_computation.4 | async-start | bytes 6291456 | tf_op jit(solution)/shard_map/all_gather | solution.py:29
  159.6 1.3 copy-start.2
  160.9 46.9 %collective-permute-start = (bf16[2048,512]{1,0:T(8,128)(2,1)S(1)}, bf16[2048,512]{1,0:T(8,128)(2,1)S(1)}, u32[]{:S(2)}, u32[]{:S(2)}) collective-permute-start(bf16[2048,512]{1,0:T(8,128)(2,1)S(1)} %fusion.16), channel_id=1, source_target_pairs={{0,64},{64,0},{1,65},{65,1},{2,66},{66,2},{3,67},{67,3},{4,68},{68... | collective-permute-start | bytes 6291464 | tf_op jit(solution)/shard_map/ppermute | solution.py:21
  207.8 1.4 copy-start.3
  236.0 140.6 %all-gather.13.cloned.1.call-start = ((), (), s32[]{:S(2)}) async-start(), calls=%async_computation.5 | async-start | bytes 6291456 | tf_op jit(solution)/shard_map/all_gather | solution.py:29
  297.7 83.9 %all-to-all-start = ((bf16[64,8,2048]{2,1,0:T(8,128)(2,1)}), bf16[64,8,2048]{2,1,0:T(8,128)(2,1)S(1)}, u32[]{:S(2)}, u32[]{:S(2)}) async-start(bf16[64,8,2048]{2,1,0:T(8,128)(2,1)} %bitcast.8), calls=%async_computation | async-start | bytes 4194304 | tf_op jit(solution)/shard_map/all_to_all | solution.py:39
  381.6 69.0 %all-to-all-start.1 = ((bf16[64,32,512]{2,1,0:T(8,128)(2,1)}), bf16[64,32,512]{2,1,0:T(8,128)(2,1)}, u32[]{:S(2)}, u32[]{:S(2)}) async-start(bf16[64,32,512]{2,1,0:T(8,128)(2,1)} %bitcast.10), calls=%async_computation.1 | async-start | bytes 4194304 | tf_op jit(solution)/shard_map/all_to_all | solution.py:39
Sparse Core Ops, SparseCore 0:
  11.2 71.6 all-gather.6
  86.0 65.0 all-gather.8
  236.2 56.4 all-gather.10
  294.1 82.4 all-gather.12
where the time goes:
time: 461 us
  waiting for transfers between devices  282 us (61%)
  matrix products  63.9 us (14%)
  blocking collectives  49.5 us (11%)
  other arithmetic  25.1 us (5%)
  starting transfers between devices  21.8 us (5%)
  between operations  15.7 us (3%)
    all_gather x2, waiting for transfers between devices, total_of_pieces(): return lax.all_gather(x, axis).astype(jnp.float32).sum(0)  111 us
    all_gather x1, waiting for transfers between devices, on_device(): lax.all_gather(w_in, FSDP, axis=0, tiled=True)  68.7 us
    all_gather x1, waiting for transfers between devices, on_device(): lax.all_gather(w_out, FSDP, axis=0, tiled=True)  54.5 us
    psum x5, blocking collectives, over_axes(): return functools.reduce(lax.psum, axes, x)  49.5 us
    ppermute x1, waiting for transfers between devices, swapped(): return lax.ppermute(block, axis, route)  46.6 us
    dot_general x1, matrix products, on_device(): lax.dot_general(normed, dpre, contract, preferred_element_type=jnp.float32)  26.8 us
    all_to_all x2, starting transfers between devices, sum_at_owner(): tiles = lax.all_to_all(in_blocks(x, dim, count), axis, 0, 0, tiled=True)  21.2 us
    dot_general x1, matrix products, on_device(): lax.dot_general(act, dpred, contract, preferred_element_type=jnp.float32)  13.9 us
  transfers between devices with their start and end apart: 7, of which 5 were waited for; matrix products, arithmetic and copies ran while one was open for 11% of the time, Pallas kernels for 0%

commit v1 on v0

--- a/solution.py
+++ b/solution.py
@@ -91,7 +91,11 @@
     act = gelu_value(pre).astype(jnp.bfloat16)
     columns = act
     output = values + jnp.dot(
-        columns, lax.all_gather(w_out, FSDP, axis=0, tiled=True), preferred_element_type=jnp.float32
+        columns,
+        jnp.concatenate(
+            lax.all_to_all(jnp.stack([w_out] * lax.axis_size(FSDP)), FSDP, 0, 0), axis=0
+        ),
+        preferred_element_type=jnp.float32,
     )
     prediction = output.astype(jnp.bfloat16)
     partner = swapped(prediction, "member", 0)

time: 461 us -> 430 us (0.933); the launches traced: 461 us -> 423 us
  waiting for transfers between devices: 282 us -> 234 us
  starting transfers between devices: 21.8 us -> 34.9 us
    ppermute x1, waiting for transfers between devices: 46.6 us -> 4.36 us  [swapped(): return lax.ppermute(block, axis, route)]
    all_to_all x0 -> x1, starting transfers between devices: none -> 12.8 us  [on_device(): lax.all_to_all(jnp.stack([w_out] * lax.axis_size(FSDP)), FSDP, 0, 0)]
    all_gather x1, waiting for transfers between devices: 54.5 us -> 47.3 us  [on_device(): lax.all_gather(w_out, FSDP, axis=0, tiled=True)]
  transfers between devices with their start and end apart: 7 -> 8, of which waited for: 5 -> 5; matrix products, arithmetic and copies ran while one was open for 11% -> 14% of each run, Pallas kernels for 0% -> 0%
where the time goes in v1:
time: 430 us; the launch traced here: 423 us
  waiting for transfers between devices  234 us (54%)
  matrix products  64.5 us (15%)
  blocking collectives  49.5 us (12%)
  starting transfers between devices  34.9 us (8%)
  other arithmetic  22.1 us (5%)
  between operations  15.9 us (4%)
    all_gather x2, waiting for transfers between devices, total_of_pieces(): return lax.all_gather(x, axis).astype(jnp.float32).sum(0)  111 us
    all_gather x1, waiting for transfers between devices, on_device(): lax.all_gather(w_in, FSDP, axis=0, tiled=True)  69.5 us
    psum x5, blocking collectives, over_axes(): return functools.reduce(lax.psum, axes, x)  49.5 us
    all_gather x1, waiting for transfers between devices, on_device(): lax.all_gather(w_out, FSDP, axis=0, tiled=True)  47.3 us
    dot_general x1, matrix products, on_device(): lax.dot_general(normed, dpre, contract, preferred_element_type=jnp.float32)  26.9 us
    all_to_all x2, starting transfers between devices, sum_at_owner(): tiles = lax.all_to_all(in_blocks(x, dim, count), axis, 0, 0, tiled=True)  21.1 us
    dot_general x1, matrix products, on_device(): lax.dot_general(act, dpred, contract, preferred_element_type=jnp.float32)  13.8 us
    dot_general x1, matrix products, on_device(): jnp.dot(columns, lax.all_gather(w_in, FSDP, axis=0, tiled=True), preferre...  13.7 us
  transfers between devices with their start and end apart: 8, of which 5 were waited for; matrix products, arithmetic and copies ran while one was open for 14% of the time, Pallas kernels for 0%

profile of v1, /device:TPU:1, one launch (start us, length us, event | category | flops | bytes accessed | tf_op | source)
XLA Modules:
  0.0 422.9 jit_solution(8554097966266283137)
XLA Ops:
  7.2 0.7 all-gather.7.cloned.1.call-update
  7.9 2.3 stack.2
  10.3 12.8 %all-to-all-start = ((bf16[64,32,512]{2,1,0:T(8,128)(2,1)}), bf16[64,32,512]{2,1,0:T(8,128)(2,1)}, u32[]{:S(2)}, u32[]{:S(2)}) async-start(bf16[64,32,512]{2,1,0:T(8,128)(2,1)} %stack.2), calls=%async_computation | async-start | bytes 4194304 | tf_op jit(solution)/shard_map/all_to_all | solution.py:96
  23.0 0.0 all-gather.9.cloned.1.call-start
  23.1 0.7 all-gather.9.cloned.1.call-update
  23.9 0.3 convert_reduce_fusion
  24.2 1.0 fusion.12
  25.3 0.1 fusion.20
  25.4 0.2 fusion.18
  25.6 69.5 %all-gather.7.cloned.1.call-done = bf16[512,2048]{1,0:T(8,128)(2,1)} async-done(((bf16[8,2048]{1,0:T(8,128)(2,1)}), bf16[512,2048]{1,0:T(8,128)(2,1)}) %all-gather.7.cloned.1.call-update) | async-done | bytes 2097168 | tf_op jit(solution)/shard_map/all_gather | solution.py:86
  95.1 13.7 %multiply_convert_fusion = (bf16[2048,2048]{1,0:T(8,128)(2,1)}, f32[2048,2048]{1,0:T(8,128)}) fusion(f32[2048]{0:T(1024)S(1)} %copy-done.4, bf16[512,2048]{1,0:T(8,128)(2,1)} %all-gather.7.cloned.1.call-done, bf16[1,2048,512]{2,1,0:T(8,128)(2,1)S(1)} %copy-done.1, f32[512]{0:T(512)S(1)} %bitcast.49, f32[512]{0:T(512)S(1)} %broadcast_add_fusion, ...), kind=kOutput, calls=%fused_computation.9 | convolution fusion | flops 4343201792 | bytes 29388800 | tf_op jit(solution)/shard_map/dot_general | solution.py:84
  108.8 9.8 %fusion.16 = bf16[2048,512]{1,0:T(8,128)(2,1)} fusion(bf16[1,2048,512]{2,1,0:T(8,128)(2,1)S(1)} %copy-done.1, bf16[2048,2048]{1,0:T(8,128)(2,1)} %get-tuple-element.4, bf16[2048,512]{1,0:T(8,128)(2,1)} %bitcast.6), kind=kOutput, calls=%fused_computation.23 | convolution fusion | flops 4298113024 | bytes 14680064 | tf_op jit(solution)/shard_map/dot_general | solution.py:93
  118.6 0.7 collective-permute-start
  119.4 47.3 %all-gather.9.cloned.1.call-done = bf16[2048,512]{1,0:T(8,128)(2,1)} async-done(((bf16[32,512]{1,0:T(8,128)(2,1)}), bf16[2048,512]{1,0:T(8,128)(2,1)}) %all-gather.9.cloned.1.call-update) | async-done | bytes 2097168 | tf_op jit(solution)/shard_map/all_gather | solution.py:112
  166.7 4.4 %collective-permute-done = bf16[2048,512]{1,0:T(8,128)(2,1)} collective-permute-done((bf16[2048,512]{1,0:T(8,128)(2,1)}, bf16[2048,512]{1,0:T(8,128)(2,1)}, u32[]{:S(2)}, u32[]{:S(2)}) %collective-permute-start) | collective-permute-done | bytes 2097184 | tf_op jit(solution)/shard_map/ppermute | solution.py:21
  171.0 26.9 %fusion.17 = bf16[512,2048]{1,0:T(8,128)(2,1)} fusion(f32[2048,2048]{1,0:T(8,128)} %get-tuple-element.5, bf16[2048,512]{1,0:T(8,128)(2,1)} %all-gather.9.cloned.1.call-done, f32[2048]{0:T(1024)S(1)} %copy-done.4, bf16[1,2048,512]{2,1,0:T(8,128)(2,1)S(1)} %copy-done.1, f32[512]{0:T(512)S(1)} %bitcast.50, f32[512]{0:T(512)S(1)} %broadcast_add_fusion, ...), kind=kOutput, calls=%fused_computation.30 | convolution fusion | flops 8697937920 | bytes 29388800 | tf_op jit(solution)/shard_map/dot_general | solution.py:118
  197.9 0.2 all-gather.13.cloned.1.call-start
  198.2 13.8 %convolution_convert_fusion = bf16[2048,512]{1,0:T(8,128)(2,1)} fusion(bf16[2048,2048]{1,0:T(8,128)(2,1)} %get-tuple-element.4, bf16[2048,512]{1,0:T(8,128)(2,1)} %param.15, bf16[2048,512]{1,0:T(8,128)(2,1)} %fusion.16, bf16[2048,512]{1,0:T(8,128)(2,1)} %collective-permute-done), kind=kOutput, calls=%fused_computation.31 | convolution fusion | flops 4312793088 | bytes 16777216 | tf_op jit(solution)/shard_map/dot_general | solution.py:119
  212.0 42.5 %all-gather.11.cloned.1.call-done = bf16[1024,2048]{1,0:T(8,128)(2,1)} async-done(((bf16[512,2048]{1,0:T(8,128)(2,1)}), bf16[1024,2048]{1,0:T(8,128)(2,1)}) %all-gather.11.cloned.1.call-update) | async-done | bytes 4194320 | tf_op jit(solution)/shard_map/all_gather | solution.py:29
  254.5 5.1 %reduce_sum.71 = bf16[512,2048]{1,0:T(8,128)(2,1)} reduce(bf16[2,512,2048]{2,1,0:T(8,128)(2,1)} %bitcast.46, bf16[]{:T(256)} %constant.28.clone.1), dimensions={0}, to_apply=%region_2.0 | reduce | flops 1048576 | bytes 6291458 | tf_op jit(solution)/shard_map/reduce_sum | solution.py:29
  259.7 10.4 %all-to-all-start.1 = ((bf16[64,8,2048]{2,1,0:T(8,128)(2,1)}), bf16[64,8,2048]{2,1,0:T(8,128)(2,1)S(1)}, u32[]{:S(2)}, u32[]{:S(2)}) async-start(bf16[64,8,2048]{2,1,0:T(8,128)(2,1)} %bitcast.9), calls=%async_computation.1 | async-start | bytes 4194304 | tf_op jit(solution)/shard_map/all_to_all | solution.py:39
  270.1 68.6 %all-gather.13.cloned.1.call-done = bf16[4096,512]{1,0:T(8,128)(2,1)} async-done(((bf16[2048,512]{1,0:T(8,128)(2,1)}), bf16[4096,512]{1,0:T(8,128)(2,1)}) %all-gather.13.cloned.1.call-update) | async-done | bytes 4194320 | tf_op jit(solution)/shard_map/all_gather | solution.py:29
  338.6 4.9 %reduce_sum.73 = bf16[2048,512]{1,0:T(8,128)(2,1)} reduce(bf16[2,2048,512]{2,1,0:T(8,128)(2,1)} %bitcast.47, bf16[]{:T(256)} %constant.28.clone.1), dimensions={0}, to_apply=%region_4.0 | reduce | flops 1048576 | bytes 6291458 | tf_op jit(solution)/shard_map/reduce_sum | solution.py:29
  343.6 10.7 %all-to-all-start.2 = ((bf16[64,32,512]{2,1,0:T(8,128)(2,1)}), bf16[64,32,512]{2,1,0:T(8,128)(2,1)}, u32[]{:S(2)}, u32[]{:S(2)}) async-start(bf16[64,32,512]{2,1,0:T(8,128)(2,1)} %bitcast.11), calls=%async_computation.2 | async-start | bytes 4194304 | tf_op jit(solution)/shard_map/all_to_all | solution.py:39
  354.3 7.1 %subtract_reduce_fusion = f32[]{:T(128)} fusion(bf16[2048,512]{1,0:T(8,128)(2,1)} %param.15, bf16[2048,512]{1,0:T(8,128)(2,1)} %fusion.16, bf16[2048,512]{1,0:T(8,128)(2,1)} %collective-permute-done), kind=kLoop, calls=%fused_computation.24 | loop fusion | flops 13631487 | bytes 6291460 | tf_op jit(solution)/shard_map/reduce_sum | solution.py:105
  361.4 16.4 %psum.35 = f32[]{:T(128)} all-reduce(f32[]{:T(128)} %subtract_reduce_fusion), channel_id=1, replica_groups=mesh['member'=2,'fsdp_0'=4,'fsdp_1'=4,'fsdp_2'=2,'fsdp_3'=2] {'member'}, use_global_device_ids=true, to_apply=%region_7.0 | all-reduce | flops 1 | bytes 8 | tf_op jit(solution)/shard_map/psum | solution.py:25
  377.8 9.4 %psum.36 = f32[]{:T(128)} all-reduce(f32[]{:T(128)} %psum.35), channel_id=1, replica_groups=mesh['member'=2,'fsdp_0'=4,'fsdp_1'=4,'fsdp_2'=2,'fsdp_3'=2] {'fsdp_0'}, use_global_device_ids=true, to_apply=%region_8.0 | all-reduce | flops 1 | bytes 8 | tf_op jit(solution)/shard_map/psum | solution.py:25
  387.1 9.0 %psum.37 = f32[]{:T(128)} all-reduce(f32[]{:T(128)} %psum.36), channel_id=1, replica_groups=mesh['member'=2,'fsdp_0'=4,'fsdp_1'=4,'fsdp_2'=2,'fsdp_3'=2] {'fsdp_1'}, use_global_device_ids=true, to_apply=%region_9.0 | all-reduce | flops 1 | bytes 8 | tf_op jit(solution)/shard_map/psum | solution.py:25
  396.2 6.2 %psum.38 = f32[]{:T(128)} all-reduce(f32[]{:T(128)} %psum.37), channel_id=1, replica_groups=mesh['member'=2,'fsdp_0'=4,'fsdp_1'=4,'fsdp_2'=2,'fsdp_3'=2] {'fsdp_2'}, use_global_device_ids=true, to_apply=%region_10.0 | all-reduce | flops 1 | bytes 8 | tf_op jit(solution)/shard_map/psum | solution.py:25
  402.4 8.5 %psum.39 = f32[]{:T(128)} all-reduce(f32[]{:T(128)} %psum.38), channel_id=1, replica_groups=mesh['member'=2,'fsdp_0'=4,'fsdp_1'=4,'fsdp_2'=2,'fsdp_3'=2] {'fsdp_3'}, use_global_device_ids=true, to_apply=%region_11.0 | all-reduce | flops 1 | bytes 8 | tf_op jit(solution)/shard_map/psum | solution.py:25
  411.6 0.9 convert_reduce_fusion.2
  412.5 2.5 convert_reduce_fusion.1
  (20 shorter events, 0.2 us)
Async XLA Ops:
  7.2 18.1 %copy-start = (f32[32,512]{1,0:T(8,128)S(1)}, f32[32,512]{1,0:T(8,128)}, u32[]{:S(2)}) copy-start(f32[32,512]{1,0:T(8,128)} %param.10) | copy-start | bytes 196612
  7.2 16.7 %copy-start.1 = (bf16[1,2048,512]{2,1,0:T(8,128)(2,1)S(1)}, bf16[1,2048,512]{2,1,0:T(8,128)(2,1)}, u32[]{:S(2)}) copy-start(bf16[1,2048,512]{2,1,0:T(8,128)(2,1)} %param.8) | copy-start | bytes 6291460
  7.2 87.9 %all-gather.7.cloned.1.call-start = ((), (), s32[]{:S(2)}) async-start(), calls=%async_computation.3 | async-start | bytes 2129920 | tf_op jit(solution)/shard_map/all_gather | solution.py:86
  10.3 15.0 %copy-start.3 = (f32[1,32]{1,0:T(1,128)S(1)}, f32[1,32]{1,0:T(1,128)}, u32[]{:S(2)}) copy-start(f32[1,32]{1,0:T(1,128)} %param.9) | copy-start | bytes 388
  10.3 15.2 %copy-start.2 = (f32[32,512]{1,0:T(8,128)S(1)}, f32[32,512]{1,0:T(8,128)}, u32[]{:S(2)}) copy-start(f32[32,512]{1,0:T(8,128)} %param.11) | copy-start | bytes 196612
  10.3 84.8 %copy-start.4 = (f32[2048]{0:T(1024)S(1)}, f32[2048]{0:T(1024)}, u32[]{:S(2)}) copy-start(f32[2048]{0:T(1024)} %param.13) | copy-start | bytes 24580
  10.3 98.5 %all-to-all-start = ((bf16[64,32,512]{2,1,0:T(8,128)(2,1)}), bf16[64,32,512]{2,1,0:T(8,128)(2,1)}, u32[]{:S(2)}, u32[]{:S(2)}) async-start(bf16[64,32,512]{2,1,0:T(8,128)(2,1)} %stack.2), calls=%async_computation | async-start | bytes 4194304 | tf_op jit(solution)/shard_map/all_to_all | solution.py:96
  23.0 143.6 %all-gather.9.cloned.1.call-start = ((), (), s32[]{:S(2)}) async-start(), calls=%async_computation.4 | async-start | bytes 2129920 | tf_op jit(solution)/shard_map/all_gather | solution.py:112
  23.8 230.7 %all-gather.11.cloned.1.call-start = ((), (), s32[]{:S(2)}) async-start(), calls=%async_computation.5 | async-start | bytes 6291456 | tf_op jit(solution)/shard_map/all_gather | solution.py:29
  118.6 52.4 %collective-permute-start = (bf16[2048,512]{1,0:T(8,128)(2,1)}, bf16[2048,512]{1,0:T(8,128)(2,1)}, u32[]{:S(2)}, u32[]{:S(2)}) collective-permute-start(bf16[2048,512]{1,0:T(8,128)(2,1)} %fusion.16), channel_id=1, source_target_pairs={{0,64},{64,0},{1,65},{65,1},{2,66},{66,2},{3,67},{67,3},{4,68},{68... | collective-permute-start | bytes 6291464 | tf_op jit(solution)/shard_map/ppermute | solution.py:21
  197.9 140.7 %all-gather.13.cloned.1.call-start = ((), (), s32[]{:S(2)}) async-start(), calls=%async_computation.6 | async-start | bytes 6291456 | tf_op jit(solution)/shard_map/all_gather | solution.py:29
  259.7 83.9 %all-to-all-start.1 = ((bf16[64,8,2048]{2,1,0:T(8,128)(2,1)}), bf16[64,8,2048]{2,1,0:T(8,128)(2,1)S(1)}, u32[]{:S(2)}, u32[]{:S(2)}) async-start(bf16[64,8,2048]{2,1,0:T(8,128)(2,1)} %bitcast.9), calls=%async_computation.1 | async-start | bytes 4194304 | tf_op jit(solution)/shard_map/all_to_all | solution.py:39
  343.6 68.9 %all-to-all-start.2 = ((bf16[64,32,512]{2,1,0:T(8,128)(2,1)}), bf16[64,32,512]{2,1,0:T(8,128)(2,1)}, u32[]{:S(2)}, u32[]{:S(2)}) async-start(bf16[64,32,512]{2,1,0:T(8,128)(2,1)} %bitcast.11), calls=%async_computation.2 | async-start | bytes 4194304 | tf_op jit(solution)/shard_map/all_to_all | solution.py:39
Sparse Core Ops, SparseCore 0:
  11.1 83.9 all-gather.6
  98.2 68.4 all-gather.8
  198.1 56.4 all-gather.10
  256.0 82.5 all-gather.12
